TPU v7x, 32 devices: a whole 2x2x4 slice. The times are simulated.
32 devices in a mesh: groups: 2 (over y), range: 8 (over z, x), sub: 2 (over core).
Axes of the slice: x: 2, y: 2, z: 4, core: 2. Of those that a mesh axis runs over, the one named last changes fastest.
Arguments:
- samples: float32 [2, 1024, 32, 128], P(None, ('groups', 'range', 'sub')), parts along dimension 1, may hold values from -6 to 6
- beam_weights: float32 [32, 8, 2, 64, 128], P(('groups', 'range'), None, None, None, 'sub'), parts along dimension 0, may hold values from -0.25 to 0.25
- subarrays: int32 [32, 8, 64], P(('groups', 'range', 'sub')), parts along dimension 0, may hold values from 0 to 511, as said below
- training: int32 [64], P(('groups', 'range', 'sub')), parts along dimension 0, may hold values 0 or 1
Outputs:
- covariance: float32 [32, 8, 64, 128], P(('groups', 'range', 'sub')), parts along dimension 0
- filtered: float32 [2, 128, 64, 128], P(None, None, ('groups', 'range', 'sub')), parts along dimension 2
- energy: float32 [256], P('groups'), parts along dimension 0
There are 2 independent parts, one for each index of `groups`. A program takes and returns all parts, laid end to end along the dimension named above; each array names one. Nothing has to cross between parts.
Inputs may be any that keep to these rules, and one draw needn't show every extreme that they name: `subarrays`: in each gate block the 512 indices are all 512 channels, each once.
All inputs are finite; a program needn't handle non-finite values. No bound on the sum of `training` on one device may be relied on, other than what follows from the above.
Results may differ from a plain program's by a relative error of at most 0.0003.
Values sent between devices are 32-bit elements; how exact they have to be, the bound alone decides.
A program may use at most 64 MiB of HBM per device.

v0:
```python
import jax
import jax.numpy as jnp
from jax import lax
from jax.sharding import PartitionSpec as P

GB = 2
loading = 0.05


def block_terms(snaps, chosen, weights, masked, factor):
    highest = lax.Precision.HIGHEST
    picked = jnp.take(snaps, chosen, axis=1)
    real_part = picked[0]
    imag_part = picked[1]
    real_masked = real_part * masked
    imag_masked = imag_part * masked
    cov_real = (
        jnp.einsum("snx,smx->snm", real_masked, real_part, precision=highest)
        + jnp.einsum("snx,smx->snm", imag_masked, imag_part, precision=highest)
    ) * factor
    cov_imag = (
        jnp.einsum("snx,smx->snm", imag_masked, real_part, precision=highest)
        - jnp.einsum("snx,smx->snm", real_masked, imag_part, precision=highest)
    ) * factor
    w_real = weights[:, 0]
    w_imag = weights[:, 1]
    out_real = jnp.einsum("snk,snx->kx", w_real, real_part, precision=highest) + jnp.einsum(
        "snk,snx->kx", w_imag, imag_part, precision=highest
    )
    out_imag = jnp.einsum("snk,snx->kx", w_real, imag_part, precision=highest) - jnp.einsum(
        "snk,snx->kx", w_imag, real_part, precision=highest
    )
    prod_real = jnp.einsum("snm,smk->snk", cov_real, w_real, precision=highest) - jnp.einsum(
        "snm,smk->snk", cov_imag, w_imag, precision=highest
    )
    prod_imag = jnp.einsum("snm,smk->snk", cov_real, w_imag, precision=highest) + jnp.einsum(
        "snm,smk->snk", cov_imag, w_real, precision=highest
    )
    quadratic = jnp.sum(w_real * prod_real + w_imag * prod_imag, axis=(0, 1))
    inverse = 1.0 / jnp.sqrt(quadratic + loading)
    filtered = jnp.stack([out_real * inverse[:, None], out_imag * inverse[:, None]])
    energy = jnp.sum(out_real * out_real + out_imag * out_imag, axis=1)
    covariance = jnp.concatenate([cov_real, cov_imag], axis=-1)
    return (covariance, filtered, energy)


def body(samples, beam_weights, subarrays, training):
    range_count = lax.axis_size("range")
    core_count = lax.axis_size("sub")
    parts_iq, chan_dev, all_gates, pulses = samples.shape
    gate_dev = all_gates // (range_count * core_count)
    channels = chan_dev * range_count * core_count
    blocks_dev = gate_dev // GB
    spread = samples.reshape(parts_iq, 1, 1, chan_dev, range_count, core_count, gate_dev, pulses)
    turned = lax.all_to_all(
        lax.all_to_all(spread, "range", split_axis=4, concat_axis=1, tiled=True),
        "sub",
        split_axis=5,
        concat_axis=2,
        tiled=True,
    )
    local_data = turned.reshape(parts_iq, channels, blocks_dev, GB * pulses).transpose(2, 0, 1, 3)
    mine = lax.all_to_all(beam_weights, "sub", split_axis=0, concat_axis=4, tiled=True)
    gates_on = training.astype(jnp.float32).reshape(blocks_dev, GB)
    masked = jnp.repeat(gates_on, pulses, axis=1)
    factor = 1.0 / (GB * pulses)
    covs, filts, energies = jax.vmap(block_terms, in_axes=(0, 0, 0, 0, None))(
        local_data, subarrays, mine, masked, factor
    )
    beams = filts.shape[2]
    filtered = filts.reshape(blocks_dev, parts_iq, beams, GB, pulses).transpose(1, 2, 0, 3, 4)
    filtered = filtered.reshape(parts_iq, beams, gate_dev, pulses)
    total = lax.psum(jnp.sum(energies, axis=0), ("range", "sub"))
    energy = total / (all_gates * pulses)
    return (covs, filtered, energy)


def solution(mesh):
    placed = (
        P(None, ("groups", "range", "sub"), None, None),
        P(("groups", "range"), None, None, None, "sub"),
        P(("groups", "range", "sub"), None, None),
        P(("groups", "range", "sub")),
    )
    return jax.shard_map(
        body,
        mesh=mesh,
        in_specs=placed,
        out_specs=(
            P(("groups", "range", "sub"), None, None, None),
            P(None, None, ("groups", "range", "sub"), None),
            P("groups"),
        ),
        check_vma=False,
    )
```

profile of v0, /device:TPU:0, one launch (start us, length us, event | category | flops | bytes accessed | tf_op | source)
XLA Modules:
  0.0 92.5 jit_solution(9004139148378862796)
XLA Ops:
  0.6 0.0 copy-start
  0.6 2.5 %reshape.157 = f32[2,1,65536]{2,1,0:T(1,128)} reshape(f32[2,8,2,64,64]{4,3,2,1,0:T(8,128)} %param.5) | data formatting | bytes 1048576
  3.2 3.5 %all-to-all-start.2 = ((f32[2,1,65536]{2,1,0:T(1,128)}), f32[2,1,65536]{2,1,0:T(1,128)S(1)}, u32[]{:S(2)}, u32[]{:S(2)}) async-start(f32[2,1,65536]{2,1,0:T(1,128)} %reshape.157), calls=%async_computation.2 | async-start | bytes 1048576 | tf_op jit(solution)/shard_map/all_to_all | solution.py:63
  6.6 0.0 copy-done
  6.7 1.6 %copy.24 = f32[2,1,1,32,8,2,2,128]{7,6,3,5,0,2,1,4:T(2,128)} copy(f32[2,1,1,32,8,2,2,128]{7,6,5,4,3,0,2,1:T(2,128)S(1)} %bitcast.103) | data formatting | bytes 2097152 | tf_op jit(solution)/shard_map/reshape | solution.py:54
  8.2 0.0 copy-start.2
  8.2 0.2 all-to-all-done.2
  8.4 0.0 copy-start.1
  8.4 7.4 %all-to-all-start = ((f32[2,1,1,32,8,2,2,128]{7,6,3,5,0,2,1,4:T(2,128)}), f32[2,1,1,32,8,2,2,128]{7,6,3,5,0,2,1,4:T(2,128)S(1)}, u32[]{:S(2)}, u32[]{:S(2)}) async-start(f32[2,1,1,32,8,2,2,128]{7,6,3,5,0,2,1,4:T(2,128)} %copy.24), calls=%async_computation | async-start | bytes 2097152 | tf_op jit(solution)/shard_map/all_to_all | solution.py:56
  15.8 0.0 copy-done.2
  15.8 0.0 copy-done.1
  15.9 0.1 reshape.147
  15.9 0.5 broadcast.75
  16.4 2.3 %reduce.5 = f32[2,65536]{1,0:T(2,128)S(1)} reduce(f32[2,1,65536]{2,1,0:T(1,128)S(1)} %all-to-all-done.2, f32[]{:T(128)} %broadcast.75), dimensions={1}, to_apply=%all_to_all.44.reduce_sub_computation | reduce | bytes 1048580 | tf_op jit(solution)/shard_map/all_to_all | solution.py:63
  18.8 0.6 reshape.158
  19.4 1.9 %copy.29 = f32[1,8,2,64,2,64]{5,4,3,1,2,0:T(2,128)} copy(f32[1,8,2,64,2,64]{5,3,2,1,4,0:T(8,128)S(1)} %bitcast.98) | data formatting | bytes 1048576 | tf_op jit(solution)/shard_map/all_to_all | solution.py:63
  21.2 1.8 %all_to_all.47 = f32[1,8,2,64,128]{4,3,1,2,0:T(8,128)S(1)} reshape(f32[1,8,2,64,2,64]{5,4,3,1,2,0:T(2,128)} %copy.29) | data formatting | bytes 1048576 | tf_op jit(solution)/shard_map/all_to_all | solution.py:63
  23.1 0.1 broadcast_bitcast_fusion
  23.1 18.9 %all-to-all-done = f32[2,1,1,32,8,2,2,128]{7,6,3,5,0,2,1,4:T(2,128)S(1)} async-done(((f32[2,1,1,32,8,2,2,128]{7,6,3,5,0,2,1,4:T(2,128)}), f32[2,1,1,32,8,2,2,128]{7,6,3,5,0,2,1,4:T(2,128)S(1)}, u32[]{:S(2)}, u32[]{:S(2)}) %all-to-all-start) | async-done | bytes 1048608 | tf_op jit(solution)/shard_map/all_to_all | solution.py:56
  42.1 0.1 copy.25
  42.1 4.6 %all_to_all.51 = f32[2,8,1,32,1,2,2,128]{7,6,3,1,0,4,2,5:T(2,128)S(1)} all-to-all(f32[2,8,1,32,1,2,2,128]{7,6,3,1,0,4,2,5:T(2,128)S(1)} %copy.25), channel_id=1, replica_groups=mesh['groups'=2,'range'=8,'sub'=2] {'sub'}, dimensions={5} | all-to-all | bytes 2097152 | tf_op jit(solution)/shard_map/all_to_all | solution.py:55
  46.7 0.1 copy.26
  46.8 0.8 copy.27
  47.6 2.3 %gather_fusion = f32[512,2,256]{2,1,0:T(2,128)S(1)} fusion(f32[1,2,512,256]{3,1,2,0:T(2,128)S(1)} %copy.27, s32[512]{0:T(512)S(1)} %reshape.147), kind=kCustom, calls=%fused_computation | custom fusion | bytes 2101248 | tf_op jit(solution)/shard_map/vmap(jit(_take))/gather | solution.py:12
  50.0 0.1 copy.28
  50.1 0.1 broadcast_select_fusion
  50.2 1.0 %convolution_bitcast_fusion.2 = f32[256,128]{1,0:T(8,128)S(1)} fusion(f32[1,2,8,64,256]{4,3,2,1,0:T(8,128)S(1)} %broadcast_select_fusion, f32[1,8,2,64,128]{4,3,1,2,0:T(8,128)S(1)} %all_to_all.47), kind=kOutput, calls=%fused_computation.13 | convolution fusion | flops 201326592 | bytes 917504 | tf_op jit(solution)/shard_map/vmap(snk,snx->kx)/dot_general | solution.py:27
  51.2 1.0 %convolution_bitcast_fusion = f32[256,128]{1,0:T(8,128)S(1)} fusion(f32[1,2,8,64,256]{4,3,2,1,0:T(8,128)S(1)} %broadcast_select_fusion, f32[1,8,2,64,128]{4,3,1,2,0:T(8,128)S(1)} %all_to_all.47), kind=kOutput, calls=%fused_computation.11 | convolution fusion | flops 201326592 | bytes 917504 | tf_op jit(solution)/shard_map/vmap(snk,snx->kx)/dot_general | solution.py:30
  52.2 0.6 fusion.12
  52.9 0.6 fusion.2
  53.5 0.4 fusion.19
  53.9 0.4 fusion.18
  54.3 0.6 fusion.8
  54.9 1.0 %fusion.6 = f32[256,128]{1,0:T(8,128)S(1)} fusion(f32[256,128]{1,0:T(8,128)S(1)} %convolution_bitcast_fusion.2, f32[1,2,8,64,256]{4,3,2,1,0:T(8,128)S(1)} %broadcast_select_fusion, f32[1,8,2,64,128]{4,3,1,2,0:T(8,128)S(1)} %all_to_all.47), kind=kOutput, calls=%fused_computation.15 | convolution fusion | flops 201359360 | bytes 1048576 | tf_op jit(solution)/shard_map/vmap(snk,snx->kx)/dot_general | solution.py:27
  55.9 0.6 fusion.3
  56.5 0.4 fusion
  56.9 0.4 fusion.5
  57.4 1.0 %add_reduce_fusion = (f32[128]{0:T(128)S(1)}, f32[256,128]{1,0:T(8,128)S(1)}, f32[256,128]{1,0:T(8,128)S(1)}) fusion(f32[256,128]{1,0:T(8,128)S(1)} %fusion.6, f32[128]{0:T(128)S(1)} %add_rsqrt_fusion, f32[256,128]{1,0:T(8,128)S(1)} %convolution_bitcast_fusion, f32[1,8,2,64,128]{4,3,1,2,0:T(8,128)S(1)} %all_to_all.47, ...), kind=kOutput, calls=%fused_computation.36 | convolution fusion | flops 201555840 | bytes 1311744 | tf_op jit(solution)/shard_map/vmap(snk,snx->kx)/dot_general | solution.py:30
  58.4 31.6 %psum.7 = f32[128]{0:T(128)S(1)} all-reduce(f32[128]{0:T(128)S(1)} %get-tuple-element.3), channel_id=1, replica_groups=mesh['groups'=2,'range'=8,'sub'=2] {'range','sub'}, use_global_device_ids=true, to_apply=%region_2.3 | all-reduce | flops 128 | bytes 1024 | tf_op jit(solution)/shard_map/psum | solution.py:73
  90.1 0.5 broadcast_multiply_fusion.2
  90.6 0.1 copy.30
  90.7 0.1 copy.31
  90.8 0.8 pad_maximum_fusion
  91.7 0.8 pad_maximum_fusion.1
  (6 shorter events, 0.0 us)
Async XLA Ops:
  0.6 6.0 %copy-start = (f32[2,32,32,128]{3,2,1,0:T(8,128)S(1)}, f32[2,32,32,128]{3,2,1,0:T(8,128)}, u32[]{:S(2)}) copy-start(f32[2,32,32,128]{3,2,1,0:T(8,128)} %param.4) | copy-start | bytes 3145732
  3.2 5.2 %all-to-all-start.2 = ((f32[2,1,65536]{2,1,0:T(1,128)}), f32[2,1,65536]{2,1,0:T(1,128)S(1)}, u32[]{:S(2)}, u32[]{:S(2)}) async-start(f32[2,1,65536]{2,1,0:T(1,128)} %reshape.157), calls=%async_computation.2 | async-start | bytes 1048576 | tf_op jit(solution)/shard_map/all_to_all | solution.py:63
  8.2 7.6 %copy-start.2 = (s32[2]{0:T(128)S(1)}, s32[2]{0:T(128)}, u32[]{:S(2)}) copy-start(s32[2]{0:T(128)} %param.7) | copy-start | bytes 28
  8.4 7.4 %copy-start.1 = (s32[1,8,64]{2,1,0:T(8,128)S(1)}, s32[1,8,64]{2,1,0:T(8,128)}, u32[]{:S(2)}) copy-start(s32[1,8,64]{2,1,0:T(8,128)} %param.6) | copy-start | bytes 6148
  8.4 33.7 %all-to-all-start = ((f32[2,1,1,32,8,2,2,128]{7,6,3,5,0,2,1,4:T(2,128)}), f32[2,1,1,32,8,2,2,128]{7,6,3,5,0,2,1,4:T(2,128)S(1)}, u32[]{:S(2)}, u32[]{:S(2)}) async-start(f32[2,1,1,32,8,2,2,128]{7,6,3,5,0,2,1,4:T(2,128)} %copy.24), calls=%async_computation | async-start | bytes 2097152 | tf_op jit(solution)/shard_map/all_to_all | solution.py:56
where the time goes:
time: 92.9 us; the launch traced here: 92.5 us
  blocking collectives  36.2 us (39%)
  waiting for transfers between devices  19.1 us (21%)
  local copies, waits for them, and re-layouts  12.7 us (14%)
  starting transfers between devices  10.9 us (12%)
  matrix products  8.13 us (9%)
  other arithmetic  4.67 us (5%)
    psum x1, blocking collectives, body(): total = lax.psum(jnp.sum(energies, axis=0), ('range', 'sub'))  31.6 us
    all_to_all x1, waiting for transfers between devices, body(): lax.all_to_all(spread, 'range', split_axis=4, concat_axis=1, tiled=True)  18.9 us
    all_to_all x1, starting transfers between devices, body(): lax.all_to_all(spread, 'range', split_axis=4, concat_axis=1, tiled=True)  7.41 us
    all_to_all x1, blocking collectives, body(): lax.all_to_all(lax.all_to_all(spread, 'range', split_axis=4, concat_axis=...  4.58 us
    all_to_all x3, local copies, waits for them, and re-layouts, body(): lax.all_to_all(beam_weights, 'sub', split_axis=0, concat_axis=4, tiled=True)  4.18 us
    all_to_all x1, starting transfers between devices, body(): lax.all_to_all(beam_weights, 'sub', split_axis=0, concat_axis=4, tiled=True)  3.49 us
    unnamed x8, local copies, waits for them, and re-layouts  3.15 us
    gather x4, local copies, waits for them, and re-layouts, block_terms(): picked = jnp.take(snaps, chosen, axis=1)  2.5 us
  transfers between devices with their start and end apart: 2, of which 2 were waited for; matrix products, arithmetic and copies ran while one was open for 8% of the time, Pallas kernels for 0%

commit v1 on v0

--- a/solution.py
+++ b/solution.py
@@ -70,7 +70,8 @@
     beams = filts.shape[2]
     filtered = filts.reshape(blocks_dev, parts_iq, beams, GB, pulses).transpose(1, 2, 0, 3, 4)
     filtered = filtered.reshape(parts_iq, beams, gate_dev, pulses)
-    total = lax.psum(jnp.sum(energies, axis=0), ("range", "sub"))
+    partial = lax.psum(jnp.sum(energies, axis=0), "sub")
+    total = lax.psum(partial, "range")
     energy = total / (all_gates * pulses)
     return (covs, filtered, energy)
 

time: 92.9 us -> 83.2 us (0.90)
  blocking collectives: 36.2 us -> 26.5 us
    psum x1 -> x2, blocking collectives: 31.6 us -> 21.9 us  [the longest x1 19.5 us: body(): total = lax.psum(partial, 'range')]
  transfers between devices with their start and end apart: 2 -> 2, of which waited for: 2 -> 2; matrix products, arithmetic and copies ran while one was open for 8% -> 9% of each run, Pallas kernels for 0% -> 0%
where the time goes in v1:
time: 83.2 us; the launch traced here: 82.8 us
  blocking collectives  26.5 us (32%)
  waiting for transfers between devices  19.1 us (23%)
  local copies, waits for them, and re-layouts  12.7 us (15%)
  starting transfers between devices  10.9 us (13%)
  matrix products  8.13 us (10%)
  other arithmetic  4.67 us (6%)
  between operations  0.84 us (1%)
    psum x1, blocking collectives, body(): total = lax.psum(partial, 'range')  19.5 us
    all_to_all x1, waiting for transfers between devices, body(): lax.all_to_all(spread, 'range', split_axis=4, concat_axis=1, tiled=True)  18.9 us
    all_to_all x1, starting transfers between devices, body(): lax.all_to_all(spread, 'range', split_axis=4, concat_axis=1, tiled=True)  7.41 us
    all_to_all x1, blocking collectives, body(): lax.all_to_all(lax.all_to_all(spread, 'range', split_axis=4, concat_axis=...  4.58 us
    all_to_all x3, local copies, waits for them, and re-layouts, body(): lax.all_to_all(beam_weights, 'sub', split_axis=0, concat_axis=4, tiled=True)  4.18 us
    all_to_all x1, starting transfers between devices, body(): lax.all_to_all(beam_weights, 'sub', split_axis=0, concat_axis=4, tiled=True)  3.49 us
    unnamed x8, local copies, waits for them, and re-layouts  3.15 us
    gather x4, local copies, waits for them, and re-layouts, block_terms(): picked = jnp.take(snaps, chosen, axis=1)  2.5 us
  transfers between devices with their start and end apart: 2, of which 2 were waited for; matrix products, arithmetic and copies ran while one was open for 9% of the time, Pallas kernels for 0%

profile of v1, /device:TPU:0, one launch (start us, length us, event | category | flops | bytes accessed | tf_op | source)
XLA Modules:
  0.0 82.8 jit_solution(17140016756013137974)
XLA Ops:
  0.6 0.0 copy-start
  0.6 2.5 %reshape.157 = f32[2,1,65536]{2,1,0:T(1,128)} reshape(f32[2,8,2,64,64]{4,3,2,1,0:T(8,128)} %param.5) | data formatting | bytes 1048576
  3.2 3.5 %all-to-all-start.2 = ((f32[2,1,65536]{2,1,0:T(1,128)}), f32[2,1,65536]{2,1,0:T(1,128)S(1)}, u32[]{:S(2)}, u32[]{:S(2)}) async-start(f32[2,1,65536]{2,1,0:T(1,128)} %reshape.157), calls=%async_computation.2 | async-start | bytes 1048576 | tf_op jit(solution)/shard_map/all_to_all | solution.py:63
  6.6 0.0 copy-done
  6.7 1.6 %copy.24 = f32[2,1,1,32,8,2,2,128]{7,6,3,5,0,2,1,4:T(2,128)} copy(f32[2,1,1,32,8,2,2,128]{7,6,5,4,3,0,2,1:T(2,128)S(1)} %bitcast.103) | data formatting | bytes 2097152 | tf_op jit(solution)/shard_map/reshape | solution.py:54
  8.2 0.0 copy-start.2
  8.2 0.2 all-to-all-done.2
  8.4 0.0 copy-start.1
  8.4 7.4 %all-to-all-start = ((f32[2,1,1,32,8,2,2,128]{7,6,3,5,0,2,1,4:T(2,128)}), f32[2,1,1,32,8,2,2,128]{7,6,3,5,0,2,1,4:T(2,128)S(1)}, u32[]{:S(2)}, u32[]{:S(2)}) async-start(f32[2,1,1,32,8,2,2,128]{7,6,3,5,0,2,1,4:T(2,128)} %copy.24), calls=%async_computation | async-start | bytes 2097152 | tf_op jit(solution)/shard_map/all_to_all | solution.py:56
  15.8 0.0 copy-done.2
  15.8 0.0 copy-done.1
  15.9 0.1 reshape.147
  15.9 0.5 broadcast.75
  16.4 2.3 %reduce.5 = f32[2,65536]{1,0:T(2,128)S(1)} reduce(f32[2,1,65536]{2,1,0:T(1,128)S(1)} %all-to-all-done.2, f32[]{:T(128)} %broadcast.75), dimensions={1}, to_apply=%all_to_all.44.reduce_sub_computation | reduce | bytes 1048580 | tf_op jit(solution)/shard_map/all_to_all | solution.py:63
  18.8 0.6 reshape.158
  19.4 1.9 %copy.29 = f32[1,8,2,64,2,64]{5,4,3,1,2,0:T(2,128)} copy(f32[1,8,2,64,2,64]{5,3,2,1,4,0:T(8,128)S(1)} %bitcast.98) | data formatting | bytes 1048576 | tf_op jit(solution)/shard_map/all_to_all | solution.py:63
  21.2 1.8 %all_to_all.47 = f32[1,8,2,64,128]{4,3,1,2,0:T(8,128)S(1)} reshape(f32[1,8,2,64,2,64]{5,4,3,1,2,0:T(2,128)} %copy.29) | data formatting | bytes 1048576 | tf_op jit(solution)/shard_map/all_to_all | solution.py:63
  23.1 0.1 broadcast_bitcast_fusion
  23.1 18.9 %all-to-all-done = f32[2,1,1,32,8,2,2,128]{7,6,3,5,0,2,1,4:T(2,128)S(1)} async-done(((f32[2,1,1,32,8,2,2,128]{7,6,3,5,0,2,1,4:T(2,128)}), f32[2,1,1,32,8,2,2,128]{7,6,3,5,0,2,1,4:T(2,128)S(1)}, u32[]{:S(2)}, u32[]{:S(2)}) %all-to-all-start) | async-done | bytes 1048608 | tf_op jit(solution)/shard_map/all_to_all | solution.py:56
  42.1 0.1 copy.25
  42.1 4.6 %all_to_all.51 = f32[2,8,1,32,1,2,2,128]{7,6,3,1,0,4,2,5:T(2,128)S(1)} all-to-all(f32[2,8,1,32,1,2,2,128]{7,6,3,1,0,4,2,5:T(2,128)S(1)} %copy.25), channel_id=1, replica_groups=mesh['groups'=2,'range'=8,'sub'=2] {'sub'}, dimensions={5} | all-to-all | bytes 2097152 | tf_op jit(solution)/shard_map/all_to_all | solution.py:55
  46.7 0.1 copy.26
  46.8 0.8 copy.27
  47.6 2.3 %gather_fusion = f32[512,2,256]{2,1,0:T(2,128)S(1)} fusion(f32[1,2,512,256]{3,1,2,0:T(2,128)S(1)} %copy.27, s32[512]{0:T(512)S(1)} %reshape.147), kind=kCustom, calls=%fused_computation | custom fusion | bytes 2101248 | tf_op jit(solution)/shard_map/vmap(jit(_take))/gather | solution.py:12
  50.0 0.1 copy.28
  50.1 0.1 broadcast_select_fusion
  50.2 1.0 %convolution_bitcast_fusion.2 = f32[256,128]{1,0:T(8,128)S(1)} fusion(f32[1,2,8,64,256]{4,3,2,1,0:T(8,128)S(1)} %broadcast_select_fusion, f32[1,8,2,64,128]{4,3,1,2,0:T(8,128)S(1)} %all_to_all.47), kind=kOutput, calls=%fused_computation.13 | convolution fusion | flops 201326592 | bytes 917504 | tf_op jit(solution)/shard_map/vmap(snk,snx->kx)/dot_general | solution.py:27
  51.2 1.0 %convolution_bitcast_fusion = f32[256,128]{1,0:T(8,128)S(1)} fusion(f32[1,2,8,64,256]{4,3,2,1,0:T(8,128)S(1)} %broadcast_select_fusion, f32[1,8,2,64,128]{4,3,1,2,0:T(8,128)S(1)} %all_to_all.47), kind=kOutput, calls=%fused_computation.11 | convolution fusion | flops 201326592 | bytes 917504 | tf_op jit(solution)/shard_map/vmap(snk,snx->kx)/dot_general | solution.py:30
  52.2 0.6 fusion.12
  52.9 0.6 fusion.2
  53.5 0.4 fusion.19
  53.9 0.4 fusion.18
  54.3 0.6 fusion.8
  54.9 1.0 %fusion.6 = f32[256,128]{1,0:T(8,128)S(1)} fusion(f32[256,128]{1,0:T(8,128)S(1)} %convolution_bitcast_fusion.2, f32[1,2,8,64,256]{4,3,2,1,0:T(8,128)S(1)} %broadcast_select_fusion, f32[1,8,2,64,128]{4,3,1,2,0:T(8,128)S(1)} %all_to_all.47), kind=kOutput, calls=%fused_computation.15 | convolution fusion | flops 201359360 | bytes 1048576 | tf_op jit(solution)/shard_map/vmap(snk,snx->kx)/dot_general | solution.py:27
  55.9 0.6 fusion.3
  56.5 0.4 fusion
  56.9 0.4 fusion.5
  57.4 1.0 %add_reduce_fusion = (f32[128]{0:T(128)S(1)}, f32[256,128]{1,0:T(8,128)S(1)}, f32[256,128]{1,0:T(8,128)S(1)}) fusion(f32[256,128]{1,0:T(8,128)S(1)} %fusion.6, f32[128]{0:T(128)S(1)} %add_rsqrt_fusion, f32[256,128]{1,0:T(8,128)S(1)} %convolution_bitcast_fusion, f32[1,8,2,64,128]{4,3,1,2,0:T(8,128)S(1)} %all_to_all.47, ...), kind=kOutput, calls=%fused_computation.36 | convolution fusion | flops 201555840 | bytes 1311744 | tf_op jit(solution)/shard_map/vmap(snk,snx->kx)/dot_general | solution.py:30
  58.4 2.5 %psum.14 = f32[128]{0:T(128)S(1)} all-reduce(f32[128]{0:T(128)S(1)} %get-tuple-element.3), channel_id=1, replica_groups=mesh['groups'=2,'range'=8,'sub'=2] {'sub'}, use_global_device_ids=true, to_apply=%region_2.3 | all-reduce | flops 128 | bytes 1024 | tf_op jit(solution)/shard_map/psum | solution.py:73
  60.9 19.5 %psum.15 = f32[128]{0:T(128)S(1)} all-reduce(f32[128]{0:T(128)S(1)} %psum.14), channel_id=1, replica_groups=mesh['groups'=2,'range'=8,'sub'=2] {'range'}, use_global_device_ids=true, to_apply=%region_3.4 | all-reduce | flops 128 | bytes 1024 | tf_op jit(solution)/shard_map/psum | solution.py:74
  80.3 0.5 broadcast_multiply_fusion.2
  80.9 0.1 copy.30
  81.0 0.1 copy.31
  81.1 0.8 %pad_maximum_fusion = f32[1,8,64,128]{3,2,1,0:T(8,128)} fusion(f32[1,8,64,64]{3,2,1,0:T(8,128)S(1)} %bitcast.102, f32[1,8,64,64]{3,2,1,0:T(8,128)S(1)} %bitcast.96), kind=kLoop, calls=%fused_computation.28 | loop fusion | flops 65536 | bytes 524288 | tf_op jit(solution)/shard_map/vmap()/concatenate | solution.py:43
  81.9 0.8 pad_maximum_fusion.1
  (6 shorter events, 0.0 us)
Async XLA Ops:
  0.6 6.0 %copy-start = (f32[2,32,32,128]{3,2,1,0:T(8,128)S(1)}, f32[2,32,32,128]{3,2,1,0:T(8,128)}, u32[]{:S(2)}) copy-start(f32[2,32,32,128]{3,2,1,0:T(8,128)} %param.4) | copy-start | bytes 3145732
  3.2 5.2 %all-to-all-start.2 = ((f32[2,1,65536]{2,1,0:T(1,128)}), f32[2,1,65536]{2,1,0:T(1,128)S(1)}, u32[]{:S(2)}, u32[]{:S(2)}) async-start(f32[2,1,65536]{2,1,0:T(1,128)} %reshape.157), calls=%async_computation.2 | async-start | bytes 1048576 | tf_op jit(solution)/shard_map/all_to_all | solution.py:63
  8.2 7.6 %copy-start.2 = (s32[2]{0:T(128)S(1)}, s32[2]{0:T(128)}, u32[]{:S(2)}) copy-start(s32[2]{0:T(128)} %param.7) | copy-start | bytes 28
  8.4 7.4 %copy-start.1 = (s32[1,8,64]{2,1,0:T(8,128)S(1)}, s32[1,8,64]{2,1,0:T(8,128)}, u32[]{:S(2)}) copy-start(s32[1,8,64]{2,1,0:T(8,128)} %param.6) | copy-start | bytes 6148
  8.4 33.7 %all-to-all-start = ((f32[2,1,1,32,8,2,2,128]{7,6,3,5,0,2,1,4:T(2,128)}), f32[2,1,1,32,8,2,2,128]{7,6,3,5,0,2,1,4:T(2,128)S(1)}, u32[]{:S(2)}, u32[]{:S(2)}) async-start(f32[2,1,1,32,8,2,2,128]{7,6,3,5,0,2,1,4:T(2,128)} %copy.24), calls=%async_computation | async-start | bytes 2097152 | tf_op jit(solution)/shard_map/all_to_all | solution.py:56
